TPU v7x, 512 devices: a whole 4x4x16 slice. The times are simulated.
512 devices in a mesh: bx: 32 (over z_hi, y, x), by: 16 (over z_lo, core).
Axes of the slice: x: 4, y: 4, z: 16 (z_hi: 2, z_lo: 8; z = z_hi * 8 + z_lo), core: 2. Of those that a mesh axis runs over, the one named last changes fastest.
Arguments:
- occ_factor: bfloat16 [32, 16, 20, 256], P('bx', 'by'), may hold values from -6 to 6
- coefficients: bfloat16 [32, 16, 9, 20, 1600], P('bx', 'by'), may hold values from -0.4375 to 0.4375
- coulomb: bfloat16 [32, 16, 9, 80, 80], P('bx', 'by'), may hold values from -0.0390625 to 0.0390625
- box_pair_mask: int32 [32, 16, 9], P('bx', 'by'), may hold values 0 or 1
- live_count: int32 [32, 16], P('bx', 'by'), may hold values from 5 to 20
Outputs:
- exchange: float32 [32, 16, 9, 20, 20], P('bx', 'by')
All inputs are finite; a program needn't handle non-finite values. No bound on the sum of `box_pair_mask` on one device may be relied on, other than what follows from the above.
Results may differ from a plain program's by a relative error of at most 0.003.
Values may be sent and summed in bfloat16 or wider, within the bound.
No kernel may reach another device: no remote copies, remote signals or barrier semaphores. Data moves between devices by JAX's collectives and lax.ppermute only.
A program may use at most 64 MiB of HBM per device.

v0:
```python
import jax
import jax.numpy as jnp
from jax import lax
from jax.sharding import PartitionSpec as P


def extended(cells, sides, width):
    for axis, dim in sides:
        count = lax.axis_size(axis)
        ends = count - 1
        head = lax.slice_in_dim(cells, 0, width, axis=dim)
        tail = lax.slice_in_dim(cells, cells.shape[dim] - width, cells.shape[dim], axis=dim)
        cells = jnp.concatenate(
            [
                lax.ppermute(tail, axis, [(i, (i + 1) % count) for i in range(ends)]),
                cells,
                lax.ppermute(head, axis, [((i + 1) % count, i) for i in range(ends)]),
            ],
            axis=dim,
        )
    return cells


def fit_boxes(coef_slots, window):
    flattened = window.reshape(window.shape[0] * window.shape[1], window.shape[2], window.shape[3])
    fitted = lax.dot_general(
        coef_slots, flattened, (((0, 1), (0, 1)), ((), ())), preferred_element_type=jnp.float32
    )
    return fitted.astype(jnp.bfloat16)


def body(occ_factor, coefficients, coulomb, box_pair_mask, live_count):
    basis_size = occ_factor.shape[2]
    orbital_count = occ_factor.shape[3]
    slot_count = coulomb.shape[2]
    aux_count = coulomb.shape[3]
    basis_rows = jnp.arange(basis_size, dtype=jnp.int32)
    row_live = (basis_rows[None, None, :, None] < live_count[:, :, None, None]).astype(jnp.float32)
    masked = (occ_factor.astype(jnp.float32) * row_live).astype(jnp.bfloat16)
    own_box_slot = (jnp.arange(slot_count, dtype=jnp.int32) == slot_count // 2).astype(jnp.int32)
    pair_on = jnp.maximum(box_pair_mask, own_box_slot[None, None, :])
    column_basis = jnp.arange(aux_count * basis_size, dtype=jnp.int32) % basis_size
    column_live = (
        column_basis[None, None, None, None, :] < live_count[:, :, None, None, None]
    ).astype(jnp.float32)
    keep_factor = pair_on[:, :, :, None, None].astype(jnp.float32) * column_live
    coef_kept = (coefficients.astype(jnp.float32) * keep_factor).astype(jnp.bfloat16)
    padded = extended(masked, (("bx", 0), ("by", 1)), 1)
    own_fit = fit_boxes(coef_kept[0, 0], padded)
    fitted_pad = extended(own_fit[None, None], (("bx", 0), ("by", 1)), 1)
    own_split = own_fit.reshape(aux_count, basis_size * orbital_count)
    blocks = []
    for neighbour_index in range(slot_count):
        row_off, col_off = divmod(neighbour_index, 3)
        nearby = fitted_pad[row_off, col_off]
        applied = jnp.dot(
            coulomb[0, 0, neighbour_index], own_split, preferred_element_type=jnp.float32
        ).astype(jnp.bfloat16)
        blocks.append(
            lax.dot_general(
                applied.reshape(aux_count, basis_size, orbital_count),
                nearby.reshape(aux_count, basis_size, orbital_count),
                (((0, 2), (0, 2)), ((), ())),
                preferred_element_type=jnp.float32,
            )
        )
    stacked = jnp.stack(blocks, axis=0)
    result = -0.25 * pair_on[0, 0][:, None, None].astype(jnp.float32) * stacked
    return result[None, None]


def solution(mesh):
    in_specs = (
        P("bx", "by", None, None),
        P("bx", "by", None, None, None),
        P("bx", "by", None, None, None),
        P("bx", "by", None),
        P("bx", "by"),
    )
    out_specs = P("bx", "by", None, None, None)
    return jax.shard_map(body, mesh=mesh, in_specs=in_specs, out_specs=out_specs, check_vma=False)
```

profile of v0, /device:TPU:31, one launch (start us, length us, event | category | flops | bytes accessed | tf_op | source)
XLA Modules:
  0.0 206.1 jit_solution(15864913739461816426)
XLA Ops:
  0.7 0.8 multiply_convert_fusion.1
  1.4 15.0 %collective-permute-start = (bf16[1,1,20,256]{3,2,1,0:T(8,128)(2,1)S(1)}, bf16[1,1,20,256]{3,2,1,0:T(8,128)(2,1)S(1)}, u32[]{:S(2)}, u32[]{:S(2)}) collective-permute-start(bf16[1,1,20,256]{3,2,1,0:T(8,128)(2,1)S(1)} %multiply_convert_fusion.1), channel_id=1, source_target_pairs={{0,16},{16,32},{32,48},{48,64},{64,80},{80,96},{96,112},{112,128},... | collective-permute-start | bytes 30728 | tf_op jit(solution)/shard_map/ppermute | solution.py:15
  16.5 1.9 collective-permute-start.1
  18.4 0.7 fusion.47
  19.1 14.8 %collective-permute-done.1 = bf16[1,1,20,256]{3,2,1,0:T(8,128)(2,1)S(1)} collective-permute-done((bf16[1,1,20,256]{3,2,1,0:T(8,128)(2,1)S(1)}, bf16[1,1,20,256]{3,2,1,0:T(8,128)(2,1)S(1)}, u32[]{:S(2)}, u32[]{:S(2)}) %collective-permute-start.1) | collective-permute-done | bytes 10272 | tf_op jit(solution)/shard_map/ppermute | solution.py:17
  33.8 4.6 %collective-permute-start.2 = (bf16[3,1,20,256]{3,2,1,0:T(8,128)(2,1)S(1)}, bf16[3,1,20,256]{3,2,1,0:T(8,128)(2,1)S(1)}, u32[]{:S(2)}, u32[]{:S(2)}) collective-permute-start(bf16[3,1,20,256]{3,2,1,0:T(8,128)(2,1)S(1)} %pad_maximum_fusion.2), channel_id=1, source_target_pairs={{0,1},{1,2},{2,3},{3,4},{4,5},{5,6},{6,7},{7,8},{8,9},{9,10},{10,1... | collective-permute-start | bytes 92168 | tf_op jit(solution)/shard_map/ppermute | solution.py:15
  38.5 1.9 collective-permute-start.3
  40.5 3.3 %collective-permute-done.3 = bf16[3,1,20,256]{3,2,1,0:T(8,128)(2,1)S(1)} collective-permute-done((bf16[3,1,20,256]{3,2,1,0:T(8,128)(2,1)S(1)}, bf16[3,1,20,256]{3,2,1,0:T(8,128)(2,1)S(1)}, u32[]{:S(2)}, u32[]{:S(2)}) %collective-permute-start.3) | collective-permute-done | bytes 30752 | tf_op jit(solution)/shard_map/ppermute | solution.py:17
  43.8 1.6 fusion.9
  45.4 1.9 collective-permute-start.4
  47.3 3.4 %collective-permute-start.5 = (bf16[1,1,1600,256]{3,2,1,0:T(8,128)(2,1)S(1)}, bf16[1,1,1600,256]{3,2,1,0:T(8,128)(2,1)S(1)}, u32[]{:S(2)}, u32[]{:S(2)}) collective-permute-start(bf16[1,1,1600,256]{3,2,1,0:T(8,128)(2,1)S(1)} %bitcast.160), channel_id=1, source_target_pairs={{16,0},{32,16},{48,32},{64,48},{80,64},{96,80},{112,96},{128,112},... | collective-permute-start | bytes 2457608 | tf_op jit(solution)/shard_map/ppermute | solution.py:17
  50.7 15.2 %collective-permute-done.4 = bf16[1,1,1600,256]{3,2,1,0:T(8,128)(2,1)S(1)} collective-permute-done((bf16[1,1,1600,256]{3,2,1,0:T(8,128)(2,1)S(1)}, bf16[1,1,1600,256]{3,2,1,0:T(8,128)(2,1)S(1)}, u32[]{:S(2)}, u32[]{:S(2)}) %collective-permute-start.4) | collective-permute-done | bytes 819232 | tf_op jit(solution)/shard_map/ppermute | solution.py:15
  65.8 14.9 %collective-permute-done.5 = bf16[1,1,1600,256]{3,2,1,0:T(8,128)(2,1)S(1)} collective-permute-done((bf16[1,1,1600,256]{3,2,1,0:T(8,128)(2,1)S(1)}, bf16[1,1,1600,256]{3,2,1,0:T(8,128)(2,1)S(1)}, u32[]{:S(2)}, u32[]{:S(2)}) %collective-permute-start.5) | collective-permute-done | bytes 819232 | tf_op jit(solution)/shard_map/ppermute | solution.py:17
  80.8 1.7 pad_maximum_fusion
  82.5 57.1 %collective-permute-start.6 = (bf16[3,1,1600,256]{3,2,1,0:T(8,128)(2,1)}, bf16[3,1,1600,256]{3,2,1,0:T(8,128)(2,1)}, u32[]{:S(2)}, u32[]{:S(2)}) collective-permute-start(bf16[3,1,1600,256]{3,2,1,0:T(8,128)(2,1)} %pad_maximum_fusion), channel_id=1, source_target_pairs={{0,1},{1,2},{2,3},{3,4},{4,5},{5,6},{6,7},{7,8},{8,9},{9,10},{10,1... | collective-permute-start | bytes 7372808 | tf_op jit(solution)/shard_map/ppermute | solution.py:15
  139.6 0.9 reshape.253
  140.5 1.3 fusion
  141.8 2.1 %collective-permute-start.7 = (bf16[3,1,1600,256]{3,2,1,0:T(8,128)(2,1)}, bf16[3,1,1600,256]{3,2,1,0:T(8,128)(2,1)}, u32[]{:S(2)}, u32[]{:S(2)}) collective-permute-start(bf16[3,1,1600,256]{3,2,1,0:T(8,128)(2,1)} %pad_maximum_fusion), channel_id=1, source_target_pairs={{1,0},{2,1},{3,2},{4,3},{5,4},{6,5},{7,6},{8,7},{9,8},{10,9},{11,1... | collective-permute-start | bytes 7372808 | tf_op jit(solution)/shard_map/ppermute | solution.py:17
  143.9 1.3 fusion.1
  145.4 1.6 reshape.254
  147.0 2.4 %reshape.255 = bf16[80,20,256]{2,1,0:T(8,128)(2,1)} reshape(bf16[80,5120]{1,0:T(8,128)(2,1)} %fusion.1) | data formatting | bytes 1638400 | tf_op jit(solution)/shard_map/reshape | solution.py:61
  149.3 1.3 fusion.2
  150.6 2.4 %reshape.256 = bf16[80,20,256]{2,1,0:T(8,128)(2,1)} reshape(bf16[80,5120]{1,0:T(8,128)(2,1)} %fusion.2) | data formatting | bytes 1638400 | tf_op jit(solution)/shard_map/reshape | solution.py:61
  153.0 1.3 fusion.3
  154.2 2.4 %reshape.257 = bf16[80,20,256]{2,1,0:T(8,128)(2,1)} reshape(bf16[80,5120]{1,0:T(8,128)(2,1)} %fusion.3) | data formatting | bytes 1638400 | tf_op jit(solution)/shard_map/reshape | solution.py:61
  156.6 1.3 fusion.4
  157.9 2.3 %reshape.258 = bf16[80,20,256]{2,1,0:T(8,128)(2,1)} reshape(bf16[80,5120]{1,0:T(8,128)(2,1)} %fusion.4) | data formatting | bytes 1638400 | tf_op jit(solution)/shard_map/reshape | solution.py:61
  160.2 1.3 fusion.5
  161.4 2.3 %reshape.259 = bf16[80,20,256]{2,1,0:T(8,128)(2,1)} reshape(bf16[80,5120]{1,0:T(8,128)(2,1)} %fusion.5) | data formatting | bytes 1638400 | tf_op jit(solution)/shard_map/reshape | solution.py:61
  163.7 1.3 fusion.6
  165.0 2.3 %reshape.260 = bf16[80,20,256]{2,1,0:T(8,128)(2,1)} reshape(bf16[80,5120]{1,0:T(8,128)(2,1)} %fusion.6) | data formatting | bytes 1638400 | tf_op jit(solution)/shard_map/reshape | solution.py:61
  167.3 1.3 fusion.7
  168.6 2.3 %reshape.261 = bf16[80,20,256]{2,1,0:T(8,128)(2,1)} reshape(bf16[80,5120]{1,0:T(8,128)(2,1)} %fusion.7) | data formatting | bytes 1638400 | tf_op jit(solution)/shard_map/reshape | solution.py:61
  170.9 1.3 fusion.8
  172.2 1.6 reshape.262
  173.8 2.1 %reshape_squeeze.25 = bf16[80,20,256]{2,1,0:T(8,128)(2,1)} reshape(bf16[1,1,1600,256]{3,2,1,0:T(8,128)(2,1)} %copy-done.13) | data formatting | bytes 1638400 | tf_op jit(solution)/shard_map/reshape;squeeze | solution.py:62
  175.9 2.1 %reshape_squeeze.30 = bf16[80,20,256]{2,1,0:T(8,128)(2,1)} reshape(bf16[1,1,1600,256]{3,2,1,0:T(8,128)(2,1)} %copy-done.14) | data formatting | bytes 1638400 | tf_op jit(solution)/shard_map/reshape;squeeze | solution.py:62
  178.0 3.1 %fusion.49 = (bf16[1,1,1600,256]{3,2,1,0:T(8,128)(2,1)}, bf16[1,1,1600,256]{3,2,1,0:T(8,128)(2,1)}, bf16[1,1,1600,256]{3,2,1,0:T(8,128)(2,1)}) fusion(bf16[3,1,1600,256]{3,2,1,0:T(8,128)(2,1)} %collective-permute-done.6), kind=kLoop, calls=%fused_computation.79 | loop fusion | bytes 4915200 | tf_op jit(solution)/shard_map/slice | solution.py:55
  181.1 2.1 %reshape_squeeze.24 = bf16[80,20,256]{2,1,0:T(8,128)(2,1)} reshape(bf16[1,1,1600,256]{3,2,1,0:T(8,128)(2,1)} %get-tuple-element.10) | data formatting | bytes 1638400 | tf_op jit(solution)/shard_map/reshape;squeeze | solution.py:62
  183.2 3.2 %fusion.48 = (bf16[1,1,1600,256]{3,2,1,0:T(8,128)(2,1)}, bf16[1,1,1600,256]{3,2,1,0:T(8,128)(2,1)}, bf16[1,1,1600,256]{3,2,1,0:T(8,128)(2,1)}) fusion(bf16[3,1,1600,256]{3,2,1,0:T(8,128)(2,1)} %collective-permute-done.7), kind=kLoop, calls=%fused_computation.78 | loop fusion | bytes 4915200 | tf_op jit(solution)/shard_map/slice | solution.py:55
  186.4 2.1 %reshape_squeeze.26 = bf16[80,20,256]{2,1,0:T(8,128)(2,1)} reshape(bf16[1,1,1600,256]{3,2,1,0:T(8,128)(2,1)} %get-tuple-element.7) | data formatting | bytes 1638400 | tf_op jit(solution)/shard_map/reshape;squeeze | solution.py:62
  188.5 2.1 %reshape_squeeze.27 = bf16[80,20,256]{2,1,0:T(8,128)(2,1)} reshape(bf16[1,1,1600,256]{3,2,1,0:T(8,128)(2,1)} %get-tuple-element.9) | data formatting | bytes 1638400 | tf_op jit(solution)/shard_map/reshape;squeeze | solution.py:62
  190.6 2.1 %reshape_squeeze.28 = bf16[80,20,256]{2,1,0:T(8,128)(2,1)} reshape(bf16[1,1,1600,256]{3,2,1,0:T(8,128)(2,1)} %get-tuple-element.6) | data formatting | bytes 1638400 | tf_op jit(solution)/shard_map/reshape;squeeze | solution.py:62
  192.7 2.1 %reshape_squeeze.29 = bf16[80,20,256]{2,1,0:T(8,128)(2,1)} reshape(bf16[1,1,1600,256]{3,2,1,0:T(8,128)(2,1)} %get-tuple-element.8) | data formatting | bytes 1638400 | tf_op jit(solution)/shard_map/reshape;squeeze | solution.py:62
  194.8 2.1 %reshape_squeeze.31 = bf16[80,20,256]{2,1,0:T(8,128)(2,1)} reshape(bf16[1,1,1600,256]{3,2,1,0:T(8,128)(2,1)} %get-tuple-element.5) | data formatting | bytes 1638400 | tf_op jit(solution)/shard_map/reshape;squeeze | solution.py:62
  196.9 1.8 fusion.18
  198.8 1.8 fusion.17
  205.3 0.7 copy.7
  (53 shorter events, 5.0 us)
Async XLA Ops:
  1.4 17.6 %collective-permute-start = (bf16[1,1,20,256]{3,2,1,0:T(8,128)(2,1)S(1)}, bf16[1,1,20,256]{3,2,1,0:T(8,128)(2,1)S(1)}, u32[]{:S(2)}, u32[]{:S(2)}) collective-permute-start(bf16[1,1,20,256]{3,2,1,0:T(8,128)(2,1)S(1)} %multiply_convert_fusion.1), channel_id=1, source_target_pairs={{0,16},{16,32},{32,48},{48,64},{64,80},{80,96},{96,112},{112,128},... | collective-permute-start | bytes 30728 | tf_op jit(solution)/shard_map/ppermute | solution.py:15
  16.5 17.4 %collective-permute-start.1 = (bf16[1,1,20,256]{3,2,1,0:T(8,128)(2,1)S(1)}, bf16[1,1,20,256]{3,2,1,0:T(8,128)(2,1)S(1)}, u32[]{:S(2)}, u32[]{:S(2)}) collective-permute-start(bf16[1,1,20,256]{3,2,1,0:T(8,128)(2,1)S(1)} %multiply_convert_fusion.1), channel_id=1, source_target_pairs={{16,0},{32,16},{48,32},{64,48},{80,64},{96,80},{112,96},{128,112},... | collective-permute-start | bytes 30728 | tf_op jit(solution)/shard_map/ppermute | solution.py:17
  33.8 6.7 %collective-permute-start.2 = (bf16[3,1,20,256]{3,2,1,0:T(8,128)(2,1)S(1)}, bf16[3,1,20,256]{3,2,1,0:T(8,128)(2,1)S(1)}, u32[]{:S(2)}, u32[]{:S(2)}) collective-permute-start(bf16[3,1,20,256]{3,2,1,0:T(8,128)(2,1)S(1)} %pad_maximum_fusion.2), channel_id=1, source_target_pairs={{0,1},{1,2},{2,3},{3,4},{4,5},{5,6},{6,7},{7,8},{8,9},{9,10},{10,1... | collective-permute-start | bytes 92168 | tf_op jit(solution)/shard_map/ppermute | solution.py:15
  38.5 5.3 %collective-permute-start.3 = (bf16[3,1,20,256]{3,2,1,0:T(8,128)(2,1)S(1)}, bf16[3,1,20,256]{3,2,1,0:T(8,128)(2,1)S(1)}, u32[]{:S(2)}, u32[]{:S(2)}) collective-permute-start(bf16[3,1,20,256]{3,2,1,0:T(8,128)(2,1)S(1)} %pad_maximum_fusion.2), channel_id=1, source_target_pairs={{1,0},{2,1},{3,2},{4,3},{5,4},{6,5},{7,6},{8,7},{9,8},{10,9},{11,1... | collective-permute-start | bytes 92168 | tf_op jit(solution)/shard_map/ppermute | solution.py:17
  45.4 94.2 %copy-start.16 = (s32[1,1,9]{2,1,0:T(1,128)S(1)}, s32[1,1,9]{2,1,0:T(1,128)}, u32[]{:S(2)}) copy-start(s32[1,1,9]{2,1,0:T(1,128)} %param.8) | copy-start | bytes 112
  45.4 20.5 %collective-permute-start.4 = (bf16[1,1,1600,256]{3,2,1,0:T(8,128)(2,1)S(1)}, bf16[1,1,1600,256]{3,2,1,0:T(8,128)(2,1)S(1)}, u32[]{:S(2)}, u32[]{:S(2)}) collective-permute-start(bf16[1,1,1600,256]{3,2,1,0:T(8,128)(2,1)S(1)} %bitcast.159), channel_id=1, source_target_pairs={{0,16},{16,32},{32,48},{48,64},{64,80},{80,96},{96,112},{112,128},... | collective-permute-start | bytes 2457608 | tf_op jit(solution)/shard_map/ppermute | solution.py:15
  47.3 33.4 %collective-permute-start.5 = (bf16[1,1,1600,256]{3,2,1,0:T(8,128)(2,1)S(1)}, bf16[1,1,1600,256]{3,2,1,0:T(8,128)(2,1)S(1)}, u32[]{:S(2)}, u32[]{:S(2)}) collective-permute-start(bf16[1,1,1600,256]{3,2,1,0:T(8,128)(2,1)S(1)} %bitcast.160), channel_id=1, source_target_pairs={{16,0},{32,16},{48,32},{64,48},{80,64},{96,80},{112,96},{128,112},... | collective-permute-start | bytes 2457608 | tf_op jit(solution)/shard_map/ppermute | solution.py:17
  65.8 16.7 %copy-start.13 = (bf16[1,1,1600,256]{3,2,1,0:T(8,128)(2,1)}, bf16[1,1,1600,256]{3,2,1,0:T(8,128)(2,1)S(1)}, u32[]{:S(2)}) copy-start(bf16[1,1,1600,256]{3,2,1,0:T(8,128)(2,1)S(1)} %collective-permute-done.4) | copy-start | bytes 2457604
  80.8 1.7 copy-start.14
  82.5 58.0 %copy-start.15 = (bf16[1,1,9,80,80]{4,3,2,1,0:T(8,128)(2,1)S(1)}, bf16[1,1,9,80,80]{4,3,2,1,0:T(8,128)(2,1)}, u32[]{:S(2)}) copy-start(bf16[1,1,9,80,80]{4,3,2,1,0:T(8,128)(2,1)} %param.7) | copy-start | bytes 345604
  82.5 95.5 %collective-permute-start.6 = (bf16[3,1,1600,256]{3,2,1,0:T(8,128)(2,1)}, bf16[3,1,1600,256]{3,2,1,0:T(8,128)(2,1)}, u32[]{:S(2)}, u32[]{:S(2)}) collective-permute-start(bf16[3,1,1600,256]{3,2,1,0:T(8,128)(2,1)} %pad_maximum_fusion), channel_id=1, source_target_pairs={{0,1},{1,2},{2,3},{3,4},{4,5},{5,6},{6,7},{7,8},{8,9},{9,10},{10,1... | collective-permute-start | bytes 7372808 | tf_op jit(solution)/shard_map/ppermute | solution.py:15
  141.8 41.4 %collective-permute-start.7 = (bf16[3,1,1600,256]{3,2,1,0:T(8,128)(2,1)}, bf16[3,1,1600,256]{3,2,1,0:T(8,128)(2,1)}, u32[]{:S(2)}, u32[]{:S(2)}) collective-permute-start(bf16[3,1,1600,256]{3,2,1,0:T(8,128)(2,1)} %pad_maximum_fusion), channel_id=1, source_target_pairs={{1,0},{2,1},{3,2},{4,3},{5,4},{6,5},{7,6},{8,7},{9,8},{10,9},{11,1... | collective-permute-start | bytes 7372808 | tf_op jit(solution)/shard_map/ppermute | solution.py:17
  196.9 1.8 copy-start.6
  196.9 3.6 %copy-start.5 = (bf16[80,20,256]{2,1,0:T(8,128)(2,1)S(1)}, bf16[80,20,256]{2,1,0:T(8,128)(2,1)}, u32[]{:S(2)}) copy-start(bf16[80,20,256]{2,1,0:T(8,128)(2,1)} %reshape.256) | copy-start | bytes 2457604
  196.9 3.7 %copy-start.12 = (bf16[80,20,256]{2,1,0:T(8,128)(2,1)S(1)}, bf16[80,20,256]{2,1,0:T(8,128)(2,1)}, u32[]{:S(2)}) copy-start(bf16[80,20,256]{2,1,0:T(8,128)(2,1)} %reshape_squeeze.26) | copy-start | bytes 2457604
  198.7 2.3 %copy-start.4 = (bf16[80,20,256]{2,1,0:T(8,128)(2,1)S(1)}, bf16[80,20,256]{2,1,0:T(8,128)(2,1)}, u32[]{:S(2)}) copy-start(bf16[80,20,256]{2,1,0:T(8,128)(2,1)} %reshape.257) | copy-start | bytes 2457604
  198.7 2.3 %copy-start.11 = (bf16[80,20,256]{2,1,0:T(8,128)(2,1)S(1)}, bf16[80,20,256]{2,1,0:T(8,128)(2,1)}, u32[]{:S(2)}) copy-start(bf16[80,20,256]{2,1,0:T(8,128)(2,1)} %reshape_squeeze.27) | copy-start | bytes 2457604
  200.6 1.2 copy-start.2
  201.0 1.3 copy-start.3
  201.1 1.6 copy-start.10
  201.8 1.3 copy-start.1
  201.8 1.6 copy-start.9
  202.6 1.3 copy-start
  202.6 1.6 copy-start.7
  203.4 1.3 copy-start.8
where the time goes:
time: 207 us; the launch traced here: 206 us
  starting transfers between devices  87.9 us (42%)
  waiting for transfers between devices  48.1 us (23%)
  local copies, waits for them, and re-layouts  46 us (22%)
  matrix products  19.7 us (10%)
  other arithmetic  3.39 us (2%)
    ppermute x4, starting transfers between devices, extended(): lax.ppermute(tail, axis, [(i, (i + 1) % count) for i in range(ends)])  78.6 us
    ppermute x4, waiting for transfers between devices, extended(): lax.ppermute(head, axis, [((i + 1) % count, i) for i in range(ends)])  32.9 us
    reshape x9, local copies, waits for them, and re-layouts, body(): applied.reshape(aux_count, basis_size, orbital_count)  19.6 us
    another operation x9, local copies, waits for them, and re-layouts, body(): nearby.reshape(aux_count, basis_size, orbital_count)  17 us
    ppermute x4, waiting for transfers between devices, extended(): lax.ppermute(tail, axis, [(i, (i + 1) % count) for i in range(ends)])  15.2 us
    dot_general x9, matrix products, body(): jnp.dot(coulomb[0, 0, neighbour_index], own_split, preferred_element_type...  11.4 us
    ppermute x4, starting transfers between devices, extended(): lax.ppermute(head, axis, [((i + 1) % count, i) for i in range(ends)])  9.29 us
    dot_general x9, matrix products, body(): lax.dot_general(applied.reshape(aux_count, basis_size, orbital_count), ne...  6.72 us
  transfers between devices with their start and end apart: 8, of which 4 were waited for; matrix products, arithmetic and copies ran while one was open for 20% of the time, Pallas kernels for 0%

commit v1 on v0

v1 whole, which is shorter than its diff:
```python
import functools

import jax
import jax.numpy as jnp
from jax import lax
from jax.experimental import pallas as pl
from jax.experimental.pallas import tpu as pltpu
from jax.sharding import PartitionSpec as P

BF = jnp.bfloat16
F32 = jnp.float32
OWN_SLOTS = (1, 3, 4, 5, 7)
GROUP = 8
VMEM = pl.BlockSpec(memory_space=pltpu.VMEM)
SMEM = pl.BlockSpec(memory_space=pltpu.SMEM)


def call(body, outs, n_smem, n_vmem, scratch, flops):
    return pl.pallas_call(
        body,
        out_shape=outs,
        in_specs=[SMEM] * n_smem + [VMEM] * n_vmem,
        out_specs=jax.tree.map(lambda _: VMEM, outs),
        scratch_shapes=scratch,
        cost_estimate=pl.CostEstimate(flops=flops, bytes_accessed=1000000, transcendentals=0),
    )


def prep_kernel(live_ref, pair_ref, coef_ref, k_ref, *rest):
    *piece_refs, kf = rest
    slots, basis, cols = coef_ref.shape
    col = lax.broadcasted_iota(jnp.int32, (1, cols), 1) % basis
    keep = (col < live_ref[0]).astype(F32)
    for s in range(slots):
        on = 1.0 if s == slots // 2 else pair_ref[s].astype(F32)
        kf[s * basis : (s + 1) * basis, :] = coef_ref[s].astype(F32) * (keep * on)
    used = slots * basis
    kf[used:, :] = jnp.zeros((kf.shape[0] - used, cols), F32)
    k_ref[...] = kf[...].astype(BF)
    at = 0
    for piece in piece_refs:
        piece[...] = kf[at : at + piece.shape[0], :].astype(BF)
        at += piece.shape[0]


def load_window(cols_refs, rows, wf, outer=None, far=None):
    basis = cols_refs[0].shape[1]
    for s in range(9):
        dr, dc = divmod(s, 3)
        if rows[dr] is None:
            block = outer[dc].astype(F32)
            block = jnp.where(far, cols_refs[dc][3].astype(F32), block)
        else:
            block = cols_refs[dc][rows[dr]].astype(F32)
        wf[s * basis : (s + 1) * basis, :] = block
    wf[9 * basis :, :] = jnp.zeros((wf.shape[0] - 9 * basis, wf.shape[1]), F32)
    return wf[...].astype(BF)


def fit_into(k_ref, window, out_ref):
    total = k_ref.shape[1]
    for at in range(0, total, 256):
        width = min(256, total - at)
        out_ref[at : at + width, :] = lax.dot_general(
            k_ref[:, at : at + width], window, (((0,), (0,)), ((), ())), preferred_element_type=F32
        ).astype(out_ref.dtype)


def own_fit_kernel(k_ref, ml_ref, mc_ref, mr_ref, c_ref, out_ref, wf):
    window = load_window((ml_ref, mc_ref, mr_ref), (0, 1, 2), wf)
    fit_into(k_ref, window, out_ref)
    total = k_ref.shape[1]
    aux = c_ref.shape[1]
    for at, (one, two) in ((total, (0, 6)), (total + aux, (2, 8))):
        out_ref[at : at + aux, :] = jnp.zeros((aux, out_ref.shape[1]), BF)
        out_ref[at : at + aux, 0:aux] = c_ref[one]
        out_ref[at : at + aux, 128 : 128 + aux] = c_ref[two]


def side_fit_kernel(rows, flag_ref, k_ref, b1_ref, b2_ref, b3_ref, ml_ref, mc_ref, mr_ref, o_ref, out_ref, wf, kk):
    far = flag_ref[0] > 0
    window = load_window((ml_ref, mc_ref, mr_ref), rows, wf, o_ref, far)

    @pl.when(far)
    def _():
        at = 0
        for piece in (b1_ref, b2_ref, b3_ref):
            kk[at : at + piece.shape[0], :] = piece[...]
            at += piece.shape[0]

    @pl.when(jnp.logical_not(far))
    def _():
        kk[...] = k_ref[...]

    fit_into(kk, window, out_ref)


def apply_into(blocks, f_ref, fs, xs):
    aux = blocks[0].shape[0]
    halves, total, lanes = fs.shape
    basis = total // aux
    for h in range(halves):
        fs[h] = f_ref[0:total, h * lanes : (h + 1) * lanes].astype(F32)
    stack = jnp.concatenate(blocks, axis=0) if len(blocks) > 1 else blocks[0]
    for m in range(basis):
        rows = pl.ds(m, aux, stride=basis)
        part = jnp.concatenate([fs.at[h][rows, :] for h in range(halves)], axis=1).astype(BF)
        res = jnp.dot(stack, part, preferred_element_type=F32)
        for t in range(len(blocks)):
            for h in range(halves):
                xs.at[t, h][rows, :] = res[t * aux : (t + 1) * aux, h * lanes : (h + 1) * lanes]


def contract(lefts, right, basis):
    step = GROUP * basis
    acc = [jnp.zeros((step, step), F32) for _ in lefts]
    for at in range(0, 1600, step):
        rhs = right(at, step)
        for i, left in enumerate(lefts):
            acc[i] = acc[i] + lax.dot_general(
                left(at, step), rhs, (((1,), (1,)), ((), ())), preferred_element_type=F32
            )
    row = lax.broadcasted_iota(jnp.int32, (step, step), 0) // basis
    col = lax.broadcasted_iota(jnp.int32, (step, step), 1) // basis
    fold = (
        lax.broadcasted_iota(jnp.int32, (step, basis), 0) % basis
        == lax.broadcasted_iota(jnp.int32, (step, basis), 1)
    ).astype(F32)
    outs = []
    for a in acc:
        a = jnp.where(row == col, a, 0.0)
        flat = a[0:basis]
        for j in range(1, GROUP):
            flat = flat + a[j * basis : (j + 1) * basis]
        outs.append(jnp.dot(flat, fold, preferred_element_type=F32, precision=lax.Precision.HIGHEST))
    return outs


def own_apply_kernel(f_ref, c_ref, x_ref, e_ref, fs, xs):
    apply_into([c_ref[s] for s in OWN_SLOTS], f_ref, fs, xs)
    for t in range(len(OWN_SLOTS)):
        for h in range(2):
            x_ref[t, :, h * 128 : (h + 1) * 128] = xs[t, h].astype(BF)
    basis = e_ref.shape[0]
    (e_ref[...],) = contract(
        [lambda at, n: x_ref[2, at : at + n, :]], lambda at, n: f_ref[at : at + n, :], basis
    )


def rows_of(ref, *lead):
    return lambda at, n: ref[(*lead, slice(at, at + n), slice(None))]


def near_apply_kernel(fl_ref, fr_ref, x_ref, xl_ref, xr_ref, el_ref, er_ref, fs, xs):
    basis = el_ref.shape[0]
    total = xl_ref.shape[1]
    aux = total // basis
    for ref, start, out in ((fl_ref, total + aux, xl_ref), (fr_ref, total, xr_ref)):
        apply_into([ref[start : start + aux, at : at + aux] for at in (0, 128)], ref, fs, xs)
        for t in range(2):
            for h in range(2):
                out[t, :, h * 128 : (h + 1) * 128] = xs[t, h].astype(BF)
    (el_ref[...],) = contract([rows_of(x_ref, 1)], rows_of(fl_ref), basis)
    (er_ref[...],) = contract([rows_of(x_ref, 3)], rows_of(fr_ref), basis)


def pairs_kernel(x_ref, xl_ref, xr_ref, up_ref, dn_ref, own_ref, lo_ref, hi_ref):
    basis = own_ref.shape[1]
    for i, (t, ref) in enumerate(((0, up_ref), (4, dn_ref))):
        own_ref[i], lo_ref[i], hi_ref[i] = contract(
            [rows_of(x_ref, t), rows_of(xl_ref, i), rows_of(xr_ref, i)], rows_of(ref), basis
        )


def join_kernel(pair_ref, left_ref, right_ref, own_ref, ec_ref, el_ref, er_ref, out_ref):
    parts = [
        left_ref[0], own_ref[0], right_ref[0], el_ref[...], ec_ref[...], er_ref[...],
        left_ref[1], own_ref[1], right_ref[1],
    ]
    for s, part in enumerate(parts):
        on = 1.0 if s == 4 else pair_ref[s].astype(F32)
        out_ref[s] = part * (-0.25 * on)


def steps(n, by, skip=None):
    return [(i, i + by) for i in range(n) if 0 <= i + by < n and {i, i + by} != skip]


def move(x, axis, pairs):
    return lax.ppermute(x, axis, pairs)


def m_kernel(live_ref, occ_ref, m_ref):
    rows = lax.broadcasted_iota(jnp.int32, occ_ref.shape, 0)
    m_ref[...] = jnp.where(rows < live_ref[0], occ_ref[...].astype(F32), 0.0).astype(BF)


def column_kernel(where_ref, up_ref, m_ref, dn_ref, edge_ref, out_ref):
    seam = edge_ref[0].astype(F32)
    out_ref[0] = jnp.where(where_ref[0] > 0, seam, up_ref[...].astype(F32)).astype(BF)
    out_ref[1] = m_ref[...]
    out_ref[2] = jnp.where(where_ref[1] > 0, seam, dn_ref[...].astype(F32)).astype(BF)
    out_ref[3] = edge_ref[1]


def body(occ_factor, coefficients, coulomb, box_pair_mask, live_count):
    basis, orbitals = occ_factor.shape[2:]
    aux = coulomb.shape[3]
    total = aux * basis
    depth = 192
    c = coulomb[0, 0]
    nx, ny = lax.axis_size("bx"), lax.axis_size("by")
    low, high = nx // 2 - 1, nx // 2
    seam = {low, high}
    sds = jax.ShapeDtypeStruct
    live, pair = live_count.reshape(1), box_pair_mask[0, 0]
    m = call(m_kernel, sds((basis, orbitals), BF), 1, 1, [], 10**5)(live, occ_factor[0, 0])
    row = lax.axis_index("bx")
    m_up = move(m, "bx", steps(nx, 1, seam))
    m_dn = move(m, "bx", steps(nx, -1, seam))
    (one, two), *relays = [(12, 19), (3, 28), (14, 17), (11, 20)]
    edge = jnp.stack([m, jnp.where(row == low, m_up, m_dn)])
    edge = move(edge, "bx", [(low, one), (high, two)])
    edge = move(edge, "bx", [(one, high), (two, low)])
    k, *kb = call(
        prep_kernel,
        (sds((depth, total), BF), *[sds((64, total), BF)] * 3),
        2, 1, [pltpu.VMEM((depth, total), F32)], 10**7,
    )(live, pair, coefficients[0, 0])
    hops = [move(kb[j], "bx", [(low, one), (high, two)]) for j, (one, two) in enumerate(relays)]
    k_up = move(k, "bx", steps(nx, 1, seam))
    k_dn = move(k, "bx", steps(nx, -1, seam))
    far = [move(hops[j], "bx", [(one, high), (two, low)]) for j, (one, two) in enumerate(relays)]
    where = jnp.stack([row == high, row == low]).astype(jnp.int32)
    column = call(column_kernel, sds((4, basis, orbitals), BF), 1, 4, [], 10**5)(where, m_up, m, m_dn, edge)
    ml = move(column, "by", steps(ny, 1))
    mr = move(column, "by", steps(ny, -1))
    windows = (ml, column, mr)
    wf = pltpu.VMEM((depth, orbitals), F32)
    fit_flops = 2 * depth * total * orbitals
    f = call(own_fit_kernel, sds((total + 2 * aux, orbitals), BF), 0, 5, [wf], fit_flops)(k, *windows, c)
    fl = move(f, "by", steps(ny, 1))
    fr = move(f, "by", steps(ny, -1))
    big = pltpu.VMEM((2, total, 128), F32)
    x, e_c = call(
        own_apply_kernel,
        (sds((5, total, orbitals), BF), sds((basis, basis), F32)),
        0, 2, [big, pltpu.VMEM((5, 2, total, 128), F32)], 10 * aux * total * orbitals,
    )(f, c)
    row = lax.axis_index("bx")
    upper = move(jnp.stack([ml[0], column[0], mr[0]]), "bx", steps(nx, 1, seam))
    lower = move(jnp.stack([ml[2], column[2], mr[2]]), "bx", steps(nx, -1, seam))
    side = []
    for rows, mine, outer, at in (((None, 0, 1), k_up, upper, high), ((1, 2, None), k_dn, lower, low)):
        flag = (row == at).astype(jnp.int32).reshape(1)
        side.append(call(
            functools.partial(side_fit_kernel, rows), sds((total, orbitals), BF), 1, 8,
            [wf, pltpu.VMEM((depth, total), BF)], fit_flops,
        )(flag, mine, *far, *windows, outer))
    xl, xr, e_l, e_r = call(
        near_apply_kernel,
        (sds((2, total, orbitals), BF),) * 2 + (sds((basis, basis), F32),) * 2,
        0, 3, [big, pltpu.VMEM((2, 2, total, 128), F32)], 10 * aux * total * orbitals,
    )(fl, fr, x)
    own, lo, hi = call(
        pairs_kernel, (sds((2, basis, basis), F32),) * 3, 0, 5, [], 10 * aux * total * orbitals,
    )(x, xl, xr, *side)
    from_right = move(lo, "by", steps(ny, -1))
    from_left = move(hi, "by", steps(ny, 1))
    out = call(
        join_kernel, sds((9, basis, basis), F32), 1, 6, [], 10**5,
    )(pair, from_left, from_right, own, e_c, e_l, e_r)
    return out[None, None]


def solution(mesh):
    in_specs = (
        P("bx", "by", None, None),
        P("bx", "by", None, None, None),
        P("bx", "by", None, None, None),
        P("bx", "by", None),
        P("bx", "by"),
    )
    out_specs = P("bx", "by", None, None, None)
    return jax.shard_map(body, mesh=mesh, in_specs=in_specs, out_specs=out_specs, check_vma=False)
```

time: 207 us -> 187 us (0.903)
  local copies, waits for them, and re-layouts: 46 us -> 7.59 us
  Pallas kernels: 0 us -> 32.8 us
  waiting for transfers between devices: 48.1 us -> 71.6 us
  matrix products: 19.7 us -> 0 us
  starting transfers between devices: 87.9 us -> 71.6 us
  other arithmetic: 3.39 us -> 1.32 us
    pallas_call x0 -> x10, Pallas kernels: none -> 32.8 us  [the longest x1 6.94 us: body(): call(pairs_kernel, (sds((2, basis, basis), F32),) * 3, 0, 5, [], 10 * aux...]
    ppermute x8 -> x20, waiting for transfers between devices: 48.1 us -> 71.6 us  [move(): return lax.ppermute(x, axis, pairs)]
    reshape x10 -> x0, local copies, waits for them, and re-layouts: 20.5 us -> none  [the longest x9 19.6 us: body(): applied.reshape(aux_count, basis_size, orbital_count)]
    dot_general x19 -> x0, matrix products: 19.7 us -> none  [the longest x9 11.4 us: body(): jnp.dot(coulomb[0, 0, neighbour_index], own_split, preferred_element_type...]
    another operation x9 -> x0, local copies, waits for them, and re-layouts: 17 us -> none  [body(): nearby.reshape(aux_count, basis_size, orbital_count)]
    ppermute x8 -> x20, starting transfers between devices: 87.9 us -> 71.6 us  [move(): return lax.ppermute(x, axis, pairs)]
    slice x2 -> x3, local copies, waits for them, and re-layouts: 6.32 us -> 2.18 us  [the longest x1 0.73 us: body(): column[2]]
    unnamed x34, local copies, waits for them, and re-layouts: 1.54 us -> 3.78 us
  transfers between devices with their start and end apart: 8 -> 20, of which waited for: 4 -> 9; matrix products, arithmetic and copies ran while one was open for 20% -> 2% of each run, Pallas kernels for 0% -> 9%
where the time goes in v1:
time: 187 us; the launch traced here: 186 us
  starting transfers between devices  71.6 us (38%)
  waiting for transfers between devices  71.6 us (38%)
  Pallas kernels  32.8 us (18%)
  local copies, waits for them, and re-layouts  7.59 us (4%)
    ppermute x20, waiting for transfers between devices, move(): return lax.ppermute(x, axis, pairs)  71.6 us
    ppermute x20, starting transfers between devices, move(): return lax.ppermute(x, axis, pairs)  71.6 us
    pallas_call x1, Pallas kernels, body(): call(pairs_kernel, (sds((2, basis, basis), F32),) * 3, 0, 5, [], 10 * aux...  6.94 us
    pallas_call x1, Pallas kernels, body(): call(near_apply_kernel, (sds((2, total, orbitals), BF),) * 2 + (sds((basi...  6.15 us
    pallas_call x2, Pallas kernels, body(): call(functools.partial(side_fit_kernel, rows), sds((total, orbitals), BF)...  5.54 us
    pallas_call x1, Pallas kernels, body(): call(own_apply_kernel, (sds((5, total, orbitals), BF), sds((basis, basis)...  5.06 us
    unnamed x34, local copies, waits for them, and re-layouts  3.78 us
  transfers between devices with their start and end apart: 20, of which 9 were waited for; matrix products, arithmetic and copies ran while one was open for 2% of the time, Pallas kernels for 9%

profile of v1, /device:TPU:31, one launch (start us, length us, event | category | flops | bytes accessed | tf_op | source)
XLA Modules:
  0.0 185.8 jit_solution(8495081350185701704)
XLA Ops:
  0.7 1.3 shard_map.56.m_ref
  2.0 1.3 collective-permute-start
  3.2 4.0 %collective-permute-start.1 = (bf16[20,256]{1,0:T(8,128)(2,1)}, bf16[20,256]{1,0:T(8,128)(2,1)S(1)}, u32[]{:S(2)}, u32[]{:S(2)}) collective-permute-start(bf16[20,256]{1,0:T(8,128)(2,1)} %shard_map.56.m_ref), channel_id=1, source_target_pairs={{16,0},{32,16},{48,32},{64,48},{80,64},{96,80},{112,96},{128,112},... | collective-permute-start | bytes 30728 | tf_op jit(solution)/shard_map/ppermute | solution.py:190
  7.3 1.0 collective-permute-done.1.dn_ref
  8.3 0.7 pad_maximum_fusion.2
  9.0 4.2 %collective-permute-start.2 = (bf16[2,20,256]{2,1,0:T(8,128)(2,1)S(1)}, bf16[2,20,256]{2,1,0:T(8,128)(2,1)S(1)}, u32[]{:S(2)}, u32[]{:S(2)}) collective-permute-start(bf16[2,20,256]{2,1,0:T(8,128)(2,1)S(1)} %pad_maximum_fusion.2), channel_id=1, source_target_pairs={{240,192},{256,304},{241,193},{257,305},{242,194},{258,306},{243,1... | collective-permute-start | bytes 61448 | tf_op jit(solution)/shard_map/ppermute | solution.py:190
  13.2 2.3 %shard_map.55 = (bf16[192,1600]{1,0:T(8,128)(2,1)}, bf16[64,1600]{1,0:T(8,128)(2,1)}, bf16[64,1600]{1,0:T(8,128)(2,1)}, bf16[64,1600]{1,0:T(8,128)(2,1)}) custom-call(s32[1]{0:T(128)} %bitcast.11.live_ref, s32[9]{0:T(128)} %bitcast.19, bf16[9,20,1600]{2,1,0:T(8,128)(2,1)} %bitcast.13), custom_call_target="tpu_custom_call" | custom-call | flops 10000000 | bytes 1000000 | tf_op jit(solution)/shard_map/pallas_call | solution.py:225
  15.6 2.0 %collective-permute-start.9 = (bf16[64,1600]{1,0:T(8,128)(2,1)}, bf16[64,1600]{1,0:T(8,128)(2,1)S(1)}, u32[]{:S(2)}, u32[]{:S(2)}) collective-permute-start(bf16[64,1600]{1,0:T(8,128)(2,1)} %get-tuple-element.22), channel_id=1, source_target_pairs={{240,48},{256,448},{241,49},{257,449},{242,50},{258,450},{243,51},... | collective-permute-start | bytes 614408 | tf_op jit(solution)/shard_map/ppermute | solution.py:190
  17.6 1.3 collective-permute-start.3
  19.5 14.6 %collective-permute-done.3.edge_ref = bf16[2,20,256]{2,1,0:T(8,128)(2,1)S(1)} collective-permute-done((bf16[2,20,256]{2,1,0:T(8,128)(2,1)S(1)}, bf16[2,20,256]{2,1,0:T(8,128)(2,1)S(1)}, u32[]{:S(2)}, u32[]{:S(2)}) %collective-permute-start.3) | collective-permute-done | bytes 20512 | tf_op jit(solution)/shard_map/ppermute | solution.py:190
  34.7 1.4 shard_map.57.mc_ref
  36.1 6.6 %collective-permute-start.4 = (bf16[4,20,256]{2,1,0:T(8,128)(2,1)}, bf16[4,20,256]{2,1,0:T(8,128)(2,1)S(1)}, u32[]{:S(2)}, u32[]{:S(2)}) collective-permute-start(bf16[4,20,256]{2,1,0:T(8,128)(2,1)} %shard_map.57.mc_ref), channel_id=1, source_target_pairs={{0,1},{1,2},{2,3},{3,4},{4,5},{5,6},{6,7},{7,8},{8,9},{9,10},{10,1... | collective-permute-start | bytes 122888 | tf_op jit(solution)/shard_map/ppermute | solution.py:190
  42.8 1.9 %collective-permute-start.5 = (bf16[4,20,256]{2,1,0:T(8,128)(2,1)}, bf16[4,20,256]{2,1,0:T(8,128)(2,1)S(1)}, u32[]{:S(2)}, u32[]{:S(2)}) collective-permute-start(bf16[4,20,256]{2,1,0:T(8,128)(2,1)} %shard_map.57.mc_ref), channel_id=1, source_target_pairs={{1,0},{2,1},{3,2},{4,3},{5,4},{6,5},{7,6},{8,7},{9,8},{10,9},{11,1... | collective-permute-start | bytes 122888 | tf_op jit(solution)/shard_map/ppermute | solution.py:190
  44.7 0.7 fusion.1
  45.5 3.0 %collective-permute-done.5.mr_ref = bf16[4,20,256]{2,1,0:T(8,128)(2,1)S(1)} collective-permute-done((bf16[4,20,256]{2,1,0:T(8,128)(2,1)}, bf16[4,20,256]{2,1,0:T(8,128)(2,1)S(1)}, u32[]{:S(2)}, u32[]{:S(2)}) %collective-permute-start.5) | collective-permute-done | bytes 40992 | tf_op jit(solution)/shard_map/ppermute | solution.py:190
  48.4 0.6 copy-done.7
  49.0 2.6 %shard_map.58.f_ref = bf16[1760,256]{1,0:T(8,128)(2,1)} custom-call(bf16[192,1600]{1,0:T(8,128)(2,1)} %get-tuple-element.18.k_ref, bf16[4,20,256]{2,1,0:T(8,128)(2,1)} %copy-done.6, bf16[4,20,256]{2,1,0:T(8,128)(2,1)} %shard_map.57.mc_ref, bf16[4,20,256]{2,1,0:T(8,128)(2,1)} %copy-done.7, bf16[9,80,80]{2,1,0:T(8,128)(2,1)} %bitcast.15), custom_call_target="tpu_custom_call" | custom-call | flops 157286400 | bytes 1000000 | tf_op jit(solution)/shard_map/pallas_call | solution.py:241
  51.6 2.0 %collective-permute-start.6 = (bf16[1760,256]{1,0:T(8,128)(2,1)}, bf16[1760,256]{1,0:T(8,128)(2,1)S(1)}, u32[]{:S(2)}, u32[]{:S(2)}) collective-permute-start(bf16[1760,256]{1,0:T(8,128)(2,1)} %shard_map.58.f_ref), channel_id=1, source_target_pairs={{0,1},{1,2},{2,3},{3,4},{4,5},{5,6},{6,7},{7,8},{8,9},{9,10},{10,1... | collective-permute-start | bytes 2703368 | tf_op jit(solution)/shard_map/ppermute | solution.py:190
  53.6 2.4 %collective-permute-start.7 = (bf16[1760,256]{1,0:T(8,128)(2,1)}, bf16[1760,256]{1,0:T(8,128)(2,1)S(1)}, u32[]{:S(2)}, u32[]{:S(2)}) collective-permute-start(bf16[1760,256]{1,0:T(8,128)(2,1)} %shard_map.58.f_ref), channel_id=1, source_target_pairs={{1,0},{2,1},{3,2},{4,3},{5,4},{6,5},{7,6},{8,7},{9,8},{10,9},{11,1... | collective-permute-start | bytes 2703368 | tf_op jit(solution)/shard_map/ppermute | solution.py:190
  56.0 0.7 fusion
  56.7 0.7 fusion.2
  57.5 1.3 collective-permute-start.15
  58.8 4.0 %collective-permute-start.11 = (bf16[64,1600]{1,0:T(8,128)(2,1)S(1)}, bf16[64,1600]{1,0:T(8,128)(2,1)S(1)}, u32[]{:S(2)}, u32[]{:S(2)}) collective-permute-start(bf16[64,1600]{1,0:T(8,128)(2,1)S(1)} %copy-done.16), channel_id=1, source_target_pairs={{240,224},{256,272},{241,225},{257,273},{242,226},{258,274},{243,2... | collective-permute-start | bytes 614408 | tf_op jit(solution)/shard_map/ppermute | solution.py:190
  62.8 2.9 %collective-permute-start.13 = (bf16[64,1600]{1,0:T(8,128)(2,1)S(1)}, bf16[64,1600]{1,0:T(8,128)(2,1)S(1)}, u32[]{:S(2)}, u32[]{:S(2)}) collective-permute-start(bf16[64,1600]{1,0:T(8,128)(2,1)S(1)} %copy-done.15), channel_id=1, source_target_pairs={{240,176},{256,320},{241,177},{257,321},{242,178},{258,322},{243,1... | collective-permute-start | bytes 614408 | tf_op jit(solution)/shard_map/ppermute | solution.py:190
  65.7 1.3 collective-permute-start.10
  67.0 0.7 collective-permute-done.11
  67.7 1.3 collective-permute-start.8
  69.0 1.1 collective-permute-done.13
  70.1 4.5 %collective-permute-start.16 = (bf16[192,1600]{1,0:T(8,128)(2,1)S(1)}, bf16[192,1600]{1,0:T(8,128)(2,1)}, u32[]{:S(2)}, u32[]{:S(2)}) collective-permute-start(bf16[192,1600]{1,0:T(8,128)(2,1)S(1)} %copy-done.5), channel_id=1, source_target_pairs={{16,0},{32,16},{48,32},{64,48},{80,64},{96,80},{112,96},{128,112},... | collective-permute-start | bytes 1843208 | tf_op jit(solution)/shard_map/ppermute | solution.py:190
  74.6 10.2 %collective-permute-done.10.b1_ref = bf16[64,1600]{1,0:T(8,128)(2,1)S(1)} collective-permute-done((bf16[64,1600]{1,0:T(8,128)(2,1)S(1)}, bf16[64,1600]{1,0:T(8,128)(2,1)S(1)}, u32[]{:S(2)}, u32[]{:S(2)}) %collective-permute-start.10) | collective-permute-done | bytes 204832 | tf_op jit(solution)/shard_map/ppermute | solution.py:190
  84.8 1.3 collective-permute-start.12
  86.1 19.0 %collective-permute-done.12.b2_ref = bf16[64,1600]{1,0:T(8,128)(2,1)S(1)} collective-permute-done((bf16[64,1600]{1,0:T(8,128)(2,1)S(1)}, bf16[64,1600]{1,0:T(8,128)(2,1)S(1)}, u32[]{:S(2)}, u32[]{:S(2)}) %collective-permute-start.12) | collective-permute-done | bytes 204832 | tf_op jit(solution)/shard_map/ppermute | solution.py:190
  105.1 1.3 collective-permute-start.14
  106.4 18.5 %collective-permute-done.14.b3_ref = bf16[64,1600]{1,0:T(8,128)(2,1)S(1)} collective-permute-done((bf16[64,1600]{1,0:T(8,128)(2,1)S(1)}, bf16[64,1600]{1,0:T(8,128)(2,1)S(1)}, u32[]{:S(2)}, u32[]{:S(2)}) %collective-permute-start.14) | collective-permute-done | bytes 204832 | tf_op jit(solution)/shard_map/ppermute | solution.py:190
  124.9 1.3 collective-permute-start.17
  126.2 5.1 %shard_map.59 = (bf16[5,1600,256]{2,1,0:T(8,128)(2,1)}, f32[20,20]{1,0:T(8,128)}) custom-call(bf16[1760,256]{1,0:T(8,128)(2,1)} %shard_map.58.f_ref, bf16[9,80,80]{2,1,0:T(8,128)(2,1)} %bitcast.16), custom_call_target="tpu_custom_call" | custom-call | flops 327680000 | bytes 1000000 | tf_op jit(solution)/shard_map/pallas_call | solution.py:245
  131.3 2.8 %shard_map.61.up_ref = bf16[1600,256]{1,0:T(8,128)(2,1)} custom-call(s32[1]{0:T(128)S(6)} %reshape.10.flag_ref, bf16[192,1600]{1,0:T(8,128)(2,1)} %collective-permute-done.8.k_ref, bf16[64,1600]{1,0:T(8,128)(2,1)} %copy-done.2, bf16[64,1600]{1,0:T(8,128)(2,1)} %copy-done.3, bf16[64,1600]{1,0:T(8,128)(2,1)} %copy-done.4, bf16[4,20,256]{2,1,0:T(8,128)(2,1)} %copy-done.6, ...), custom_call_target="tpu_custom_call" | custom-call | flops 157286400 | bytes 1000000 | tf_op jit(solution)/shard_map/pallas_call | solution.py:256
  134.1 0.6 copy-done.11
  134.7 2.8 %shard_map.62.dn_ref = bf16[1600,256]{1,0:T(8,128)(2,1)} custom-call(s32[1]{0:T(128)S(6)} %reshape.11.flag_ref, bf16[192,1600]{1,0:T(8,128)(2,1)} %collective-permute-done.16.k_ref, bf16[64,1600]{1,0:T(8,128)(2,1)} %copy-done.2, bf16[64,1600]{1,0:T(8,128)(2,1)} %copy-done.3, bf16[64,1600]{1,0:T(8,128)(2,1)} %copy-done.4, bf16[4,20,256]{2,1,0:T(8,128)(2,1)} %copy-done.6, ...), custom_call_target="tpu_custom_call" | custom-call | flops 157286400 | bytes 1000000 | tf_op jit(solution)/shard_map/pallas_call | solution.py:256
  137.5 1.0 copy-done
  138.8 6.2 %shard_map.60 = (bf16[2,1600,256]{2,1,0:T(8,128)(2,1)}, bf16[2,1600,256]{2,1,0:T(8,128)(2,1)}, f32[20,20]{1,0:T(8,128)}, f32[20,20]{1,0:T(8,128)}) custom-call(bf16[1760,256]{1,0:T(8,128)(2,1)} %copy-done, bf16[1760,256]{1,0:T(8,128)(2,1)} %copy-done.1, bf16[5,1600,256]{2,1,0:T(8,128)(2,1)} %get-tuple-element.19.x_ref), custom_call_target="tpu_custom_call" | custom-call | flops 327680000 | bytes 1000000 | tf_op jit(solution)/shard_map/pallas_call | solution.py:260
  144.9 6.9 %shard_map.63 = (f32[2,20,20]{2,1,0:T(8,128)}, f32[2,20,20]{2,1,0:T(8,128)}, f32[2,20,20]{2,1,0:T(8,128)}) custom-call(bf16[5,1600,256]{2,1,0:T(8,128)(2,1)} %get-tuple-element.19.x_ref, bf16[2,1600,256]{2,1,0:T(8,128)(2,1)} %get-tuple-element.20.xl_ref, bf16[2,1600,256]{2,1,0:T(8,128)(2,1)} %get-tuple-element.21.xr_ref, ...), custom_call_target="tpu_custom_call" | custom-call | flops 327680000 | bytes 1000000 | tf_op jit(solution)/shard_map/pallas_call | solution.py:265
  151.9 24.9 %collective-permute-start.18 = (f32[2,20,20]{2,1,0:T(8,128)}, f32[2,20,20]{2,1,0:T(8,128)S(1)}, u32[]{:S(2)}, u32[]{:S(2)}) collective-permute-start(f32[2,20,20]{2,1,0:T(8,128)} %get-tuple-element.25), channel_id=1, source_target_pairs={{0,1},{1,2},{2,3},{3,4},{4,5},{5,6},{6,7},{7,8},{8,9},{9,10},{10,1... | collective-permute-start | bytes 9608 | tf_op jit(solution)/shard_map/ppermute | solution.py:190
  176.8 1.9 %collective-permute-start.19 = (f32[2,20,20]{2,1,0:T(8,128)}, f32[2,20,20]{2,1,0:T(8,128)S(1)}, u32[]{:S(2)}, u32[]{:S(2)}) collective-permute-start(f32[2,20,20]{2,1,0:T(8,128)} %get-tuple-element.26), channel_id=1, source_target_pairs={{1,0},{2,1},{3,2},{4,3},{5,4},{6,5},{7,6},{8,7},{9,8},{10,9},{11,1... | collective-permute-start | bytes 9608 | tf_op jit(solution)/shard_map/ppermute | solution.py:190
  178.7 3.4 %collective-permute-done.19.right_ref = f32[2,20,20]{2,1,0:T(8,128)S(1)} collective-permute-done((f32[2,20,20]{2,1,0:T(8,128)}, f32[2,20,20]{2,1,0:T(8,128)S(1)}, u32[]{:S(2)}, u32[]{:S(2)}) %collective-permute-start.19) | collective-permute-done | bytes 3232 | tf_op jit(solution)/shard_map/ppermute | solution.py:190
  182.1 0.6 copy-done.13
  182.8 1.4 shard_map.64
  184.2 1.6 copy.6
  (45 shorter events, 1.6 us)
Async XLA Ops:
  2.0 5.3 %collective-permute-start = (bf16[20,256]{1,0:T(8,128)(2,1)}, bf16[20,256]{1,0:T(8,128)(2,1)S(1)}, u32[]{:S(2)}, u32[]{:S(2)}) collective-permute-start(bf16[20,256]{1,0:T(8,128)(2,1)} %shard_map.56.m_ref), channel_id=1, source_target_pairs={{0,16},{16,32},{32,48},{48,64},{64,80},{80,96},{96,112},{112,128},... | collective-permute-start | bytes 30728 | tf_op jit(solution)/shard_map/ppermute | solution.py:190
  3.2 5.0 %collective-permute-start.1 = (bf16[20,256]{1,0:T(8,128)(2,1)}, bf16[20,256]{1,0:T(8,128)(2,1)S(1)}, u32[]{:S(2)}, u32[]{:S(2)}) collective-permute-start(bf16[20,256]{1,0:T(8,128)(2,1)} %shard_map.56.m_ref), channel_id=1, source_target_pairs={{16,0},{32,16},{48,32},{64,48},{80,64},{96,80},{112,96},{128,112},... | collective-permute-start | bytes 30728 | tf_op jit(solution)/shard_map/ppermute | solution.py:190
  7.3 26.8 %copy-start.8 = (bf16[20,256]{1,0:T(8,128)(2,1)}, bf16[20,256]{1,0:T(8,128)(2,1)S(1)}, u32[]{:S(2)}) copy-start(bf16[20,256]{1,0:T(8,128)(2,1)S(1)} %collective-permute-done.up_ref) | copy-start | bytes 30724
  8.3 25.8 %copy-start.9 = (bf16[20,256]{1,0:T(8,128)(2,1)}, bf16[20,256]{1,0:T(8,128)(2,1)S(1)}, u32[]{:S(2)}) copy-start(bf16[20,256]{1,0:T(8,128)(2,1)S(1)} %collective-permute-done.1.dn_ref) | copy-start | bytes 30724
  9.0 8.6 %collective-permute-start.2 = (bf16[2,20,256]{2,1,0:T(8,128)(2,1)S(1)}, bf16[2,20,256]{2,1,0:T(8,128)(2,1)S(1)}, u32[]{:S(2)}, u32[]{:S(2)}) collective-permute-start(bf16[2,20,256]{2,1,0:T(8,128)(2,1)S(1)} %pad_maximum_fusion.2), channel_id=1, source_target_pairs={{240,192},{256,304},{241,193},{257,305},{242,194},{258,306},{243,1... | collective-permute-start | bytes 61448 | tf_op jit(solution)/shard_map/ppermute | solution.py:190
  15.5 43.2 %copy-start.16 = (bf16[64,1600]{1,0:T(8,128)(2,1)S(1)}, bf16[64,1600]{1,0:T(8,128)(2,1)}, u32[]{:S(2)}) copy-start(bf16[64,1600]{1,0:T(8,128)(2,1)} %get-tuple-element.23) | copy-start | bytes 614404
  15.6 47.3 %copy-start.15 = (bf16[64,1600]{1,0:T(8,128)(2,1)S(1)}, bf16[64,1600]{1,0:T(8,128)(2,1)}, u32[]{:S(2)}) copy-start(bf16[64,1600]{1,0:T(8,128)(2,1)} %get-tuple-element.24) | copy-start | bytes 614404
  15.6 52.2 %copy-start.5 = (bf16[192,1600]{1,0:T(8,128)(2,1)S(1)}, bf16[192,1600]{1,0:T(8,128)(2,1)}, u32[]{:S(2)}) copy-start(bf16[192,1600]{1,0:T(8,128)(2,1)} %get-tuple-element.18.k_ref) | copy-start | bytes 1843204
  15.6 50.1 %collective-permute-start.9 = (bf16[64,1600]{1,0:T(8,128)(2,1)}, bf16[64,1600]{1,0:T(8,128)(2,1)S(1)}, u32[]{:S(2)}, u32[]{:S(2)}) collective-permute-start(bf16[64,1600]{1,0:T(8,128)(2,1)} %get-tuple-element.22), channel_id=1, source_target_pairs={{240,48},{256,448},{241,49},{257,449},{242,50},{258,450},{243,51},... | collective-permute-start | bytes 614408 | tf_op jit(solution)/shard_map/ppermute | solution.py:190
  17.6 16.5 %collective-permute-start.3 = (bf16[2,20,256]{2,1,0:T(8,128)(2,1)S(1)}, bf16[2,20,256]{2,1,0:T(8,128)(2,1)S(1)}, u32[]{:S(2)}, u32[]{:S(2)}) collective-permute-start(bf16[2,20,256]{2,1,0:T(8,128)(2,1)S(1)} %collective-permute-done.2), channel_id=1, source_target_pairs={{192,256},{304,240},{193,257},{305,241},{194,258},{306,242},{195,2... | collective-permute-start | bytes 61448 | tf_op jit(solution)/shard_map/ppermute | solution.py:190
  34.1 0.6 copy-start.14
  36.1 9.3 %collective-permute-start.4 = (bf16[4,20,256]{2,1,0:T(8,128)(2,1)}, bf16[4,20,256]{2,1,0:T(8,128)(2,1)S(1)}, u32[]{:S(2)}, u32[]{:S(2)}) collective-permute-start(bf16[4,20,256]{2,1,0:T(8,128)(2,1)} %shard_map.57.mc_ref), channel_id=1, source_target_pairs={{0,1},{1,2},{2,3},{3,4},{4,5},{5,6},{6,7},{7,8},{8,9},{9,10},{10,1... | collective-permute-start | bytes 122888 | tf_op jit(solution)/shard_map/ppermute | solution.py:190
  42.8 5.6 %collective-permute-start.5 = (bf16[4,20,256]{2,1,0:T(8,128)(2,1)}, bf16[4,20,256]{2,1,0:T(8,128)(2,1)S(1)}, u32[]{:S(2)}, u32[]{:S(2)}) collective-permute-start(bf16[4,20,256]{2,1,0:T(8,128)(2,1)} %shard_map.57.mc_ref), channel_id=1, source_target_pairs={{1,0},{2,1},{3,2},{4,3},{5,4},{6,5},{7,6},{8,7},{9,8},{10,9},{11,1... | collective-permute-start | bytes 122888 | tf_op jit(solution)/shard_map/ppermute | solution.py:190
  45.5 3.0 %copy-start.6 = (bf16[4,20,256]{2,1,0:T(8,128)(2,1)}, bf16[4,20,256]{2,1,0:T(8,128)(2,1)S(1)}, u32[]{:S(2)}) copy-start(bf16[4,20,256]{2,1,0:T(8,128)(2,1)S(1)} %collective-permute-done.4.ml_ref) | copy-start | bytes 122884
  48.4 0.6 copy-start.7
  51.6 85.8 %collective-permute-start.6 = (bf16[1760,256]{1,0:T(8,128)(2,1)}, bf16[1760,256]{1,0:T(8,128)(2,1)S(1)}, u32[]{:S(2)}, u32[]{:S(2)}) collective-permute-start(bf16[1760,256]{1,0:T(8,128)(2,1)} %shard_map.58.f_ref), channel_id=1, source_target_pairs={{0,1},{1,2},{2,3},{3,4},{4,5},{5,6},{6,7},{7,8},{8,9},{9,10},{10,1... | collective-permute-start | bytes 2703368 | tf_op jit(solution)/shard_map/ppermute | solution.py:190
  53.6 83.8 %collective-permute-start.7 = (bf16[1760,256]{1,0:T(8,128)(2,1)}, bf16[1760,256]{1,0:T(8,128)(2,1)S(1)}, u32[]{:S(2)}, u32[]{:S(2)}) collective-permute-start(bf16[1760,256]{1,0:T(8,128)(2,1)} %shard_map.58.f_ref), channel_id=1, source_target_pairs={{1,0},{2,1},{3,2},{4,3},{5,4},{6,5},{7,6},{8,7},{9,8},{10,9},{11,1... | collective-permute-start | bytes 2703368 | tf_op jit(solution)/shard_map/ppermute | solution.py:190
  57.5 5.3 %collective-permute-start.15 = (bf16[3,20,256]{2,1,0:T(8,128)(2,1)S(1)}, bf16[3,20,256]{2,1,0:T(8,128)(2,1)S(1)}, u32[]{:S(2)}, u32[]{:S(2)}) collective-permute-start(bf16[3,20,256]{2,1,0:T(8,128)(2,1)S(1)} %pad_maximum_fusion), channel_id=1, source_target_pairs={{0,16},{16,32},{32,48},{48,64},{64,80},{80,96},{96,112},{112,128},... | collective-permute-start | bytes 92168 | tf_op jit(solution)/shard_map/ppermute | solution.py:190
  58.8 8.9 %collective-permute-start.11 = (bf16[64,1600]{1,0:T(8,128)(2,1)S(1)}, bf16[64,1600]{1,0:T(8,128)(2,1)S(1)}, u32[]{:S(2)}, u32[]{:S(2)}) collective-permute-start(bf16[64,1600]{1,0:T(8,128)(2,1)S(1)} %copy-done.16), channel_id=1, source_target_pairs={{240,224},{256,272},{241,225},{257,273},{242,226},{258,274},{243,2... | collective-permute-start | bytes 614408 | tf_op jit(solution)/shard_map/ppermute | solution.py:190
  62.8 68.5 %copy-start.10 = (bf16[3,20,256]{2,1,0:T(8,128)(2,1)}, bf16[3,20,256]{2,1,0:T(8,128)(2,1)S(1)}, u32[]{:S(2)}) copy-start(bf16[3,20,256]{2,1,0:T(8,128)(2,1)S(1)} %collective-permute-done.15.o_ref) | copy-start | bytes 92164
  62.8 7.3 %collective-permute-start.13 = (bf16[64,1600]{1,0:T(8,128)(2,1)S(1)}, bf16[64,1600]{1,0:T(8,128)(2,1)S(1)}, u32[]{:S(2)}, u32[]{:S(2)}) collective-permute-start(bf16[64,1600]{1,0:T(8,128)(2,1)S(1)} %copy-done.15), channel_id=1, source_target_pairs={{240,176},{256,320},{241,177},{257,321},{242,178},{258,322},{243,1... | collective-permute-start | bytes 614408 | tf_op jit(solution)/shard_map/ppermute | solution.py:190
  65.7 19.1 %collective-permute-start.10 = (bf16[64,1600]{1,0:T(8,128)(2,1)S(1)}, bf16[64,1600]{1,0:T(8,128)(2,1)S(1)}, u32[]{:S(2)}, u32[]{:S(2)}) collective-permute-start(bf16[64,1600]{1,0:T(8,128)(2,1)S(1)} %collective-permute-done.9), channel_id=1, source_target_pairs={{48,256},{448,240},{49,257},{449,241},{50,258},{450,242},{51,259},... | collective-permute-start | bytes 614408 | tf_op jit(solution)/shard_map/ppermute | solution.py:190
  67.7 63.6 %collective-permute-start.8 = (bf16[192,1600]{1,0:T(8,128)(2,1)S(1)}, bf16[192,1600]{1,0:T(8,128)(2,1)}, u32[]{:S(2)}, u32[]{:S(2)}) collective-permute-start(bf16[192,1600]{1,0:T(8,128)(2,1)S(1)} %copy-done.5), channel_id=1, source_target_pairs={{0,16},{16,32},{32,48},{48,64},{64,80},{80,96},{96,112},{112,128},... | collective-permute-start | bytes 1843208 | tf_op jit(solution)/shard_map/ppermute | solution.py:190
  70.1 64.0 %collective-permute-start.16 = (bf16[192,1600]{1,0:T(8,128)(2,1)S(1)}, bf16[192,1600]{1,0:T(8,128)(2,1)}, u32[]{:S(2)}, u32[]{:S(2)}) collective-permute-start(bf16[192,1600]{1,0:T(8,128)(2,1)S(1)} %copy-done.5), channel_id=1, source_target_pairs={{16,0},{32,16},{48,32},{64,48},{80,64},{96,80},{112,96},{128,112},... | collective-permute-start | bytes 1843208 | tf_op jit(solution)/shard_map/ppermute | solution.py:190
  84.8 46.5 %copy-start.2 = (bf16[64,1600]{1,0:T(8,128)(2,1)}, bf16[64,1600]{1,0:T(8,128)(2,1)S(1)}, u32[]{:S(2)}) copy-start(bf16[64,1600]{1,0:T(8,128)(2,1)S(1)} %collective-permute-done.10.b1_ref) | copy-start | bytes 614404
  84.8 20.3 %collective-permute-start.12 = (bf16[64,1600]{1,0:T(8,128)(2,1)S(1)}, bf16[64,1600]{1,0:T(8,128)(2,1)S(1)}, u32[]{:S(2)}, u32[]{:S(2)}) collective-permute-start(bf16[64,1600]{1,0:T(8,128)(2,1)S(1)} %collective-permute-done.11), channel_id=1, source_target_pairs={{224,256},{272,240},{225,257},{273,241},{226,258},{274,242},{227,2... | collective-permute-start | bytes 614408 | tf_op jit(solution)/shard_map/ppermute | solution.py:190
  105.1 26.2 %copy-start.3 = (bf16[64,1600]{1,0:T(8,128)(2,1)}, bf16[64,1600]{1,0:T(8,128)(2,1)S(1)}, u32[]{:S(2)}) copy-start(bf16[64,1600]{1,0:T(8,128)(2,1)S(1)} %collective-permute-done.12.b2_ref) | copy-start | bytes 614404
  105.1 19.8 %collective-permute-start.14 = (bf16[64,1600]{1,0:T(8,128)(2,1)S(1)}, bf16[64,1600]{1,0:T(8,128)(2,1)S(1)}, u32[]{:S(2)}, u32[]{:S(2)}) collective-permute-start(bf16[64,1600]{1,0:T(8,128)(2,1)S(1)} %collective-permute-done.13), channel_id=1, source_target_pairs={{176,256},{320,240},{177,257},{321,241},{178,258},{322,242},{179,2... | collective-permute-start | bytes 614408 | tf_op jit(solution)/shard_map/ppermute | solution.py:190
  124.9 6.4 %copy-start.4 = (bf16[64,1600]{1,0:T(8,128)(2,1)}, bf16[64,1600]{1,0:T(8,128)(2,1)S(1)}, u32[]{:S(2)}) copy-start(bf16[64,1600]{1,0:T(8,128)(2,1)S(1)} %collective-permute-done.14.b3_ref) | copy-start | bytes 614404
  124.9 9.2 %collective-permute-start.17 = (bf16[3,20,256]{2,1,0:T(8,128)(2,1)S(1)}, bf16[3,20,256]{2,1,0:T(8,128)(2,1)S(1)}, u32[]{:S(2)}, u32[]{:S(2)}) collective-permute-start(bf16[3,20,256]{2,1,0:T(8,128)(2,1)S(1)} %pad_maximum_fusion.1), channel_id=1, source_target_pairs={{16,0},{32,16},{48,32},{64,48},{80,64},{96,80},{112,96},{128,112},... | collective-permute-start | bytes 92168 | tf_op jit(solution)/shard_map/ppermute | solution.py:190
  134.1 0.6 copy-start.11
  137.5 1.0 copy-start
  137.5 1.3 copy-start.1
  151.9 26.8 %collective-permute-start.18 = (f32[2,20,20]{2,1,0:T(8,128)}, f32[2,20,20]{2,1,0:T(8,128)S(1)}, u32[]{:S(2)}, u32[]{:S(2)}) collective-permute-start(f32[2,20,20]{2,1,0:T(8,128)} %get-tuple-element.25), channel_id=1, source_target_pairs={{0,1},{1,2},{2,3},{3,4},{4,5},{5,6},{6,7},{7,8},{8,9},{9,10},{10,1... | collective-permute-start | bytes 9608 | tf_op jit(solution)/shard_map/ppermute | solution.py:190
  176.8 5.4 %collective-permute-start.19 = (f32[2,20,20]{2,1,0:T(8,128)}, f32[2,20,20]{2,1,0:T(8,128)S(1)}, u32[]{:S(2)}, u32[]{:S(2)}) collective-permute-start(f32[2,20,20]{2,1,0:T(8,128)} %get-tuple-element.26), channel_id=1, source_target_pairs={{1,0},{2,1},{3,2},{4,3},{5,4},{6,5},{7,6},{8,7},{9,8},{10,9},{11,1... | collective-permute-start | bytes 9608 | tf_op jit(solution)/shard_map/ppermute | solution.py:190
  178.7 3.4 %copy-start.12 = (f32[2,20,20]{2,1,0:T(8,128)}, f32[2,20,20]{2,1,0:T(8,128)S(1)}, u32[]{:S(2)}) copy-start(f32[2,20,20]{2,1,0:T(8,128)S(1)} %collective-permute-done.18.left_ref) | copy-start | bytes 9604
  182.1 0.6 copy-start.13
